TPU v7x, 32 devices: a whole 2x2x4 slice. The times are simulated.
32 devices in a mesh: dp: 8 (over z, x), head: 4 (over y, core).
Axes of the slice: x: 2, y: 2, z: 4, core: 2. Of those that a mesh axis runs over, the one named last changes fastest.
Arguments:
- inputs: bfloat16 [16384, 1024], P(('dp', 'head')), may hold values from -6 to 6
- lengths: int32 [8, 4], P('dp'), may hold values from 1 to 1024, 2048 in all within a row
- attn_gain: bfloat16 [1024], replicated, may hold values from 0.5 to 1.5
- attn_shift: bfloat16 [1024], replicated, may hold values from -3 to 3
- mlp_gain: bfloat16 [1024], replicated, may hold values from 0.5 to 1.5
- mlp_shift: bfloat16 [1024], replicated, may hold values from -3 to 3
- w_qkv: bfloat16 [1024, 3072], replicated, may hold values from -0.1875 to 0.1875
- b_qkv: bfloat16 [3072], replicated, may hold values from -3 to 3
- w_out: bfloat16 [1024, 1024], replicated, may hold values from -1.5 to 1.5
- b_out: bfloat16 [1024], replicated, may hold values from -3 to 3
- w_up: bfloat16 [1024, 4096], replicated, may hold values from -0.1875 to 0.1875
- b_up: bfloat16 [4096], replicated, may hold values from -3 to 3
- w_down: bfloat16 [4096, 1024], replicated, may hold values from -0.09375 to 0.09375
- b_down: bfloat16 [1024], replicated, may hold values from -3 to 3
- cotangent: bfloat16 [16384, 1024], P(('dp', 'head')), may hold values from -6 to 6
Outputs:
- output: bfloat16 [16384, 1024], P(('dp', 'head'))
- grad_inputs: float32 [16384, 1024], P(('dp', 'head'))
- grad_attn_gain: float32 [1024], replicated
- grad_attn_shift: float32 [1024], replicated
- grad_mlp_gain: float32 [1024], replicated
- grad_mlp_shift: float32 [1024], replicated
- grad_w_qkv: float32 [1024, 3072], P('dp', 'head')
- grad_b_qkv: float32 [3072], replicated
- grad_w_out: float32 [1024, 1024], P('dp', 'head')
- grad_b_out: float32 [1024], replicated
- grad_w_up: float32 [1024, 4096], P('dp', 'head')
- grad_b_up: float32 [4096], replicated
- grad_w_down: float32 [4096, 1024], P('dp', 'head')
- grad_b_down: float32 [1024], replicated
Inputs may be any that keep to these rules, and one draw needn't show every extreme that they name: Each row lists the lengths of the 4 sequences packed in order into one group of 2048 tokens; a row sums to 2048 and its longest sequence has 1024 tokens.
All inputs are finite; a program needn't handle non-finite values.
Results may differ from a plain program's by a relative error of at most 0.012.
Values may be sent and summed in bfloat16 or wider, within the bound.
A program may use at most 192 MiB of HBM per device.

v0:
```python
import jax
import jax.numpy as jnp
from jax import lax
from jax.sharding import PartitionSpec as P

HD = 64
ROT = 16


def layer_norm(value, gain, shift):
    center = value - jnp.mean(value, axis=-1, keepdims=True)
    scale_inv = lax.rsqrt(jnp.mean(center * center, axis=-1, keepdims=True) + 1e-05)
    normed = center * scale_inv
    return (normed * gain + shift, normed, scale_inv)


def norm_back(grad_norm, normed, scale_inv, gain):
    grad_hat = grad_norm * gain
    grad_value = scale_inv * (
        grad_hat
        - jnp.mean(grad_hat, axis=-1, keepdims=True)
        - normed * jnp.mean(grad_hat * normed, axis=-1, keepdims=True)
    )
    return (grad_value, jnp.sum(grad_norm * normed, axis=0), jnp.sum(grad_norm, axis=0))


def group_layout(seq_lens, total_len):
    seq_ends = jnp.cumsum(seq_lens, dtype=jnp.int32)
    starts = seq_ends - seq_lens
    index = jnp.arange(total_len, dtype=jnp.int32)
    segment = jnp.sum(
        (index[:, None] >= seq_ends[None, :]).astype(jnp.int32), axis=1, dtype=jnp.int32
    )
    chosen = segment[:, None] == jnp.arange(seq_lens.shape[0], dtype=jnp.int32)[None, :]
    offset = jnp.sum(jnp.where(chosen, starts[None, :], 0), axis=1, dtype=jnp.int32)
    return (segment, index - offset)


def rotate(value, position, sign):
    half_rot = ROT // 2
    freqs = 10000.0 ** (-(2.0 * jnp.arange(half_rot, dtype=jnp.float32)) / ROT)
    angles = position.astype(jnp.float32)[:, None] * freqs[None, :]
    cosine = jnp.cos(angles)[:, None, :]
    sine = jnp.sin(angles)[:, None, :]
    first = value[..., :half_rot]
    second = value[..., half_rot:ROT]
    return jnp.concatenate(
        [
            first * cosine - sign * second * sine,
            second * cosine + sign * first * sine,
            value[..., ROT:],
        ],
        axis=-1,
    )


def block_scores(queries, keys_rot, segment, start, block):
    query_blk = lax.dynamic_slice_in_dim(queries, start, block, 0)
    row_seg = lax.dynamic_slice_in_dim(segment, start, block, 0)
    row_index = start + jnp.arange(block, dtype=jnp.int32)
    key_index = jnp.arange(keys_rot.shape[0], dtype=jnp.int32)
    scores = jnp.einsum(
        "qhd,khd->hqk", query_blk, keys_rot, preferred_element_type=jnp.float32
    ) * HD ** (-0.5)
    allowed = (row_seg[:, None] == segment[None, :]) & (key_index[None, :] <= row_index[:, None])
    return (jnp.where(allowed[None], scores, -1e30), query_blk)


def body(
    inputs,
    lengths,
    attn_gain,
    attn_shift,
    mlp_gain,
    mlp_shift,
    w_qkv,
    b_qkv,
    w_out,
    b_out,
    w_up,
    b_up,
    w_down,
    b_down,
    cotangent,
):
    tok_rows = inputs.shape[0]
    width = inputs.shape[1]
    in_float = inputs.astype(jnp.float32)
    gain_attn = attn_gain.astype(jnp.float32)
    gain_mlp = mlp_gain.astype(jnp.float32)
    norm_attn, normed_attn, inv_attn = layer_norm(
        in_float, gain_attn, attn_shift.astype(jnp.float32)
    )
    norm_mlp, normed_mlp, inv_mlp = layer_norm(in_float, gain_mlp, mlp_shift.astype(jnp.float32))
    norm_attn = norm_attn.astype(jnp.bfloat16)
    norm_mlp = norm_mlp.astype(jnp.bfloat16)
    triple = (
        jnp.dot(norm_attn, w_qkv, preferred_element_type=jnp.float32) + b_qkv.astype(jnp.float32)
    ).astype(jnp.bfloat16)
    triple_heads = lax.all_to_all(
        triple.reshape(tok_rows, 3, width), "head", split_axis=2, concat_axis=0, tiled=True
    )
    group_rows = triple_heads.shape[0]
    local_width = triple_heads.shape[2]
    local_heads = local_width // HD
    segment, position = group_layout(lengths[0], group_rows)
    queries = rotate(
        triple_heads[:, 0].astype(jnp.float32).reshape(group_rows, local_heads, HD), position, 1.0
    ).astype(jnp.bfloat16)
    keys_rot = rotate(
        triple_heads[:, 1].astype(jnp.float32).reshape(group_rows, local_heads, HD), position, 1.0
    ).astype(jnp.bfloat16)
    values = triple_heads[:, 2].reshape(group_rows, local_heads, HD)
    block = min(512, group_rows)
    blocks = group_rows // block

    def forward_block(block_id):
        scores, unused = block_scores(queries, keys_rot, segment, block_id * block, block)
        peak = jnp.max(scores, axis=-1, keepdims=True)
        weights = jnp.exp(scores - peak)
        totals = jnp.sum(weights, axis=-1, keepdims=True)
        probs = (weights / totals).astype(jnp.bfloat16)
        out_blk = jnp.einsum("hqk,khd->qhd", probs, values, preferred_element_type=jnp.float32)
        return (out_blk.astype(jnp.bfloat16), (peak + jnp.log(totals))[..., 0])

    context_blocks, log_totals = lax.map(forward_block, jnp.arange(blocks, dtype=jnp.int32))
    context_heads = context_blocks.reshape(group_rows, local_width)
    context = lax.all_to_all(context_heads, "head", split_axis=0, concat_axis=1, tiled=True)
    attn_part = jnp.dot(context, w_out, preferred_element_type=jnp.float32) + b_out.astype(
        jnp.float32
    )
    pre_act = jnp.dot(norm_mlp, w_up, preferred_element_type=jnp.float32) + b_up.astype(jnp.float32)
    gelu_value, gelu_pull = jax.vjp(lambda value: jax.nn.gelu(value, approximate=False), pre_act)
    hidden = gelu_value.astype(jnp.bfloat16)
    mlp_part = jnp.dot(hidden, w_down, preferred_element_type=jnp.float32) + b_down.astype(
        jnp.float32
    )
    output = (in_float + attn_part + mlp_part).astype(jnp.bfloat16)
    grad_float = cotangent.astype(jnp.float32)
    grad_w_down = jnp.einsum("tf,td->fd", hidden, cotangent, preferred_element_type=jnp.float32)
    grad_hidden = jnp.einsum("td,fd->tf", cotangent, w_down, preferred_element_type=jnp.float32)
    grad_pre = gelu_pull(grad_hidden)[0].astype(jnp.bfloat16)
    grad_w_up = jnp.einsum("td,tf->df", norm_mlp, grad_pre, preferred_element_type=jnp.float32)
    grad_norm_mlp = jnp.einsum("tf,df->td", grad_pre, w_up, preferred_element_type=jnp.float32)
    grad_w_out = jnp.einsum("td,te->de", context, cotangent, preferred_element_type=jnp.float32)
    grad_context = jnp.einsum(
        "te,de->td", cotangent, w_out, preferred_element_type=jnp.float32
    ).astype(jnp.bfloat16)
    grad_ctx_heads = lax.all_to_all(grad_context, "head", split_axis=1, concat_axis=0, tiled=True)
    grad_ctx_heads = grad_ctx_heads.reshape(group_rows, local_heads, HD)
    scale = HD ** (-0.5)

    def backward_block(carry, block_id):
        grad_keys, grad_values = carry
        start = block_id * block
        scores, query_blk = block_scores(queries, keys_rot, segment, start, block)
        probs = jnp.exp(scores - log_totals[block_id][:, :, None])
        probs_low = probs.astype(jnp.bfloat16)
        grad_out_blk = lax.dynamic_slice_in_dim(grad_ctx_heads, start, block, 0)
        grad_values = grad_values + jnp.einsum(
            "hqk,qhd->khd", probs_low, grad_out_blk, preferred_element_type=jnp.float32
        )
        grad_probs = jnp.einsum(
            "qhd,khd->hqk", grad_out_blk, values, preferred_element_type=jnp.float32
        )
        inner = jnp.sum(probs * grad_probs, axis=-1, keepdims=True)
        grad_scores = (probs * (grad_probs - inner)).astype(jnp.bfloat16)
        grad_query = (
            jnp.einsum("hqk,khd->qhd", grad_scores, keys_rot, preferred_element_type=jnp.float32)
            * scale
        )
        grad_keys = (
            grad_keys
            + jnp.einsum("hqk,qhd->khd", grad_scores, query_blk, preferred_element_type=jnp.float32)
            * scale
        )
        return ((grad_keys, grad_values), grad_query)

    zeros_kv = jnp.zeros((group_rows, local_heads, HD), jnp.float32)
    (grad_keys, grad_values), grad_queries = lax.scan(
        backward_block, (zeros_kv, zeros_kv), jnp.arange(blocks, dtype=jnp.int32)
    )
    grad_queries = rotate(grad_queries.reshape(group_rows, local_heads, HD), position, -1.0)
    grad_keys = rotate(grad_keys, position, -1.0)
    grad_heads = (
        jnp.stack([grad_queries, grad_keys, grad_values], axis=1)
        .reshape(group_rows, 3, local_width)
        .astype(jnp.bfloat16)
    )
    grad_triple = lax.all_to_all(
        grad_heads, "head", split_axis=0, concat_axis=2, tiled=True
    ).reshape(tok_rows, 3 * width)
    grad_w_qkv = jnp.einsum("td,te->de", norm_attn, grad_triple, preferred_element_type=jnp.float32)
    grad_norm_attn = jnp.einsum("te,de->td", grad_triple, w_qkv, preferred_element_type=jnp.float32)
    grad_x_attn, grad_gain_attn, grad_shift_attn = norm_back(
        grad_norm_attn, normed_attn, inv_attn, gain_attn
    )
    grad_x_mlp, grad_gain_mlp, grad_shift_mlp = norm_back(
        grad_norm_mlp, normed_mlp, inv_mlp, gain_mlp
    )
    grad_inputs = grad_float + grad_x_attn + grad_x_mlp
    column_sum = jnp.sum(grad_float, axis=0)
    summed = lax.psum(
        (
            grad_gain_attn,
            grad_shift_attn,
            grad_gain_mlp,
            grad_shift_mlp,
            jnp.sum(grad_triple.astype(jnp.float32), axis=0),
            column_sum,
            jnp.sum(grad_pre.astype(jnp.float32), axis=0),
        ),
        ("dp", "head"),
    )
    matrices = (grad_w_qkv, grad_w_out, grad_w_up, grad_w_down)
    partial_rows = (
        lax.psum_scatter(matrices[0], "dp", scatter_dimension=0, tiled=True),
        lax.psum_scatter(matrices[1], "dp", scatter_dimension=0, tiled=True),
        lax.psum_scatter(matrices[2], "dp", scatter_dimension=0, tiled=True),
        lax.psum_scatter(matrices[3], "dp", scatter_dimension=0, tiled=True),
    )
    finals = (
        lax.psum_scatter(partial_rows[0], "head", scatter_dimension=1, tiled=True),
        lax.psum_scatter(partial_rows[1], "head", scatter_dimension=1, tiled=True),
        lax.psum_scatter(partial_rows[2], "head", scatter_dimension=1, tiled=True),
        lax.psum_scatter(partial_rows[3], "head", scatter_dimension=1, tiled=True),
    )
    return (
        output,
        grad_inputs,
        summed[0],
        summed[1],
        summed[2],
        summed[3],
        finals[0],
        summed[4],
        finals[1],
        summed[5],
        finals[2],
        summed[6],
        finals[3],
        summed[5],
    )


def solution(mesh):
    return jax.shard_map(
        body,
        mesh=mesh,
        in_specs=(
            P(("dp", "head"), None),
            P("dp", None),
            P(),
            P(),
            P(),
            P(),
            P(),
            P(),
            P(),
            P(),
            P(),
            P(),
            P(),
            P(),
            P(("dp", "head"), None),
        ),
        out_specs=(
            P(("dp", "head"), None),
            P(("dp", "head"), None),
            P(),
            P(),
            P(),
            P(),
            P("dp", "head"),
            P(),
            P("dp", "head"),
            P(),
            P("dp", "head"),
            P(),
            P("dp", "head"),
            P(),
        ),
        check_vma=False,
    )
```

profile of v0, /device:TPU:0, one launch (start us, length us, event | category | flops | bytes accessed | tf_op | source)
XLA Modules:
  0.0 1508.9 jit_solution(16333594497788970276)
XLA Ops:
  40.9 45.1 %all-to-all-done = bf16[512,3,1024]{0,1,2:T(4,128)(2,1)} async-done(((bf16[512,3,1024]{0,1,2:T(4,128)(2,1)}), bf16[512,3,1024]{0,1,2:T(4,128)(2,1)}, u32[]{:S(2)}, u32[]{:S(2)}) %all-to-all-start) | async-done | bytes 3145760 | tf_op jit(solution)/shard_map/all_to_all | solution.py:100
  117.6 69.1 %while.27 = (s32[]{:T(128)}, bf16[4,512,4,64]{1,3,2,0:T(8,128)(2,1)}, f32[4,4,512]{2,1,0:T(4,128)S(1)}, s32[4]{0:T(128)S(1)}, s32[2048]{0:T(1024)S(1)}, /*index=...) while((s32[]{:T(128)}, ...), condition=%wide.region_8.9_spmd, body=%wide.region_5.0_spmd.sunk | while | flops 1127348736 | bytes 61426396 | solution.py:126
  210.3 306.1 %while.28 = (s32[]{:T(128)}, f32[2048,4,64]{0,2,1:T(8,128)}, f32[2048,4,64]{0,2,1:T(8,128)}, f32[4,512,4,64]{1,0,3,2:T(4,128)}, s32[4]{0:T(128)S(1)}, /*index=5*...) while((s32[]{:T(128)}, f32[2048,4,64]{0,2,1:T(8,128)}, ...), condition=%wide.region_11.12_spmd.clone, body=%wide.region_9.11_spmd.clone.sunk | while | flops 2753165824 | bytes 187246960 | solution.py:180
  225.4 14.8 multiply_reduce_fusion.4
  240.2 12.4 multiply_convert_fusion.3
  257.1 11.1 dynamic_update_slice.20
  274.8 12.1 fusion.149
  301.4 14.8 multiply_reduce_fusion.4
  316.2 12.1 multiply_convert_fusion.3
  351.0 12.4 fusion.149
  377.9 14.8 multiply_reduce_fusion.4
  392.6 12.1 multiply_convert_fusion.3
  427.4 12.4 fusion.149
  454.3 14.8 multiply_reduce_fusion.4
  469.1 12.1 multiply_convert_fusion.3
  503.9 12.4 fusion.149
  535.6 51.9 %all_to_all.68 = bf16[2048,3,256]{2,1,0:T(4,128)(2,1)S(1)} all-to-all(bf16[2048,3,256]{2,1,0:T(4,128)(2,1)} %copy.93), channel_id=1, replica_groups=mesh['dp'=8,'head'=4] {'head'}, dimensions={0} | all-to-all | bytes 6291456 | tf_op jit(solution)/shard_map/all_to_all | solution.py:190
  612.0 28.6 %convert_reduce_fusion = (f32[4096]{0:T(1024)S(1)}, bf16[512,4096]{1,0:T(8,128)(2,1)}, f32[512,4096]{1,0:T(8,128)}) fusion(f32[512,4096]{1,0:T(8,128)S(1)} %fusion.73, f32[4096]{0:T(1024)S(1)} %convert_element_type.119, bf16[512,1024]{1,0:T(8,128)(2,1)S(1)} %copy-done.10, bf16[4096,1024]{1,0:T(8,128)(2,1)} %param.31), kind=kOutput, calls=%fused_computation.49 | convolution fusion | flops 4452249600 | bytes 30441472 | tf_op jit(solution)/shard_map/td,fd->tf/dot_general | solution.py:141
  672.6 140.0 %reduce-scatter.9.cloned.1.call-done = f32[128,3072]{1,0:T(8,128)} async-done(((f32[1024,3072]{1,0:T(8,128)}), f32[128,3072]{1,0:T(8,128)}) %reduce-scatter.9.cloned.1.call-update) | async-done | bytes 1572880 | tf_op jit(solution)/shard_map/reduce_scatter | solution.py:217
  812.7 282.6 %reduce-scatter.21.cloned.1.call-done = f32[512,1024]{1,0:T(8,128)} async-done(((f32[4096,1024]{1,0:T(8,128)}), f32[512,1024]{1,0:T(8,128)}) %reduce-scatter.21.cloned.1.call-update) | async-done | bytes 2097168 | tf_op jit(solution)/shard_map/reduce_scatter | solution.py:220
  1105.9 271.7 %reduce-scatter.17.cloned.1.call-done = f32[128,4096]{1,0:T(8,128)} async-done(((f32[1024,4096]{1,0:T(8,128)}), f32[128,4096]{1,0:T(8,128)}) %reduce-scatter.17.cloned.1.call-update) | async-done | bytes 2097168 | tf_op jit(solution)/shard_map/reduce_scatter | solution.py:219
  1399.5 40.4 %all-reduce = (f32[1024]{0:T(1024)}, f32[1024]{0:T(1024)}, f32[1024]{0:T(1024)}, f32[1024]{0:T(1024)}, f32[3072]{0:T(1024)}, /*index=5*/f32[1024]{0:T(1024)S(1)}, f32[4096]{0:T(1024)}) all-reduce(f32[1024]{0:T(1024)S(1)} %get-tuple-element.189, f32[1024]{0:T(1024)S(1)} %get-tuple-element.194, ...), channel_id=1, replica_groups=mesh['dp'=8,'head'=4] {'dp','head'}, use_global_device_ids=true, to_apply=%region_17.18 | all-reduce | flops 12288 | bytes 98304 | tf_op jit(solution)/shard_map/psum | solution.py:203
  1439.9 26.8 %reduce-scatter.23.cloned.1.call-done = f32[512,256]{1,0:T(8,128)} async-done(((f32[512,1024]{1,0:T(8,128)}), f32[512,256]{1,0:T(8,128)}) %reduce-scatter.23.cloned.1.call-update) | async-done | bytes 524304 | tf_op jit(solution)/shard_map/reduce_scatter | solution.py:226
  1466.7 34.3 %reduce-scatter.19.cloned.1.call-done = f32[128,1024]{1,0:T(8,128)} async-done(((f32[128,4096]{1,0:T(8,128)}), f32[128,1024]{1,0:T(8,128)}) %reduce-scatter.19.cloned.1.call-update) | async-done | bytes 524304 | tf_op jit(solution)/shard_map/reduce_scatter | solution.py:225
  (256 shorter events, 390.4 us)
Async XLA Ops:
  7.2 30.2 %copy-start = (bf16[1024,1024]{1,0:T(8,128)(2,1)S(1)}, bf16[1024,1024]{1,0:T(8,128)(2,1)}, u32[]{:S(2)}) copy-start(bf16[1024,1024]{1,0:T(8,128)(2,1)} %param.27) | copy-start | bytes 6291460
  32.1 53.9 %all-to-all-start = ((bf16[512,3,1024]{0,1,2:T(4,128)(2,1)}), bf16[512,3,1024]{0,1,2:T(4,128)(2,1)}, u32[]{:S(2)}, u32[]{:S(2)}) async-start(bf16[512,3,1024]{0,1,2:T(4,128)(2,1)} %copy.84), calls=%async_computation | async-start | bytes 8388608 | tf_op jit(solution)/shard_map/all_to_all | solution.py:100
  40.9 72.8 %copy-start.12 = (f32[2048,8]{0,1:T(8,128)}, f32[2048,8]{0,1:T(8,128)S(1)}, u32[]{:S(2)}) copy-start(f32[2048,8]{0,1:T(8,128)S(1)} %get-tuple-element.272) | copy-start | bytes 196612
  86.0 100.7 %all-to-all-start.2 = ((bf16[512,4,256]{2,0,1:T(8,128)(2,1)}), bf16[512,4,256]{2,0,1:T(8,128)(2,1)}, u32[]{:S(2)}, u32[]{:S(2)}) async-start(bf16[512,4,256]{2,0,1:T(8,128)(2,1)} %bitcast.89), calls=%async_computation.2 | async-start | bytes 2097152 | tf_op jit(solution)/shard_map/all_to_all | solution.py:149
  186.7 18.8 %all-to-all-start.1 = ((bf16[4,512,256]{1,2,0:T(8,128)(2,1)}), bf16[4,512,256]{1,2,0:T(8,128)(2,1)}, u32[]{:S(2)}, u32[]{:S(2)}) async-start(bf16[4,512,256]{1,2,0:T(8,128)(2,1)} %bitcast.15), calls=%async_computation.1 | async-start | bytes 2097152 | tf_op jit(solution)/shard_map/all_to_all | solution.py:128
  190.9 481.1 %reduce-scatter.13.cloned.1.call-start = ((), (), s32[]{:S(2)}) async-start(), calls=%async_computation.14 | async-start | bytes 4718592 | tf_op jit(solution)/shard_map/reduce_scatter | solution.py:218
  210.2 602.4 %reduce-scatter.9.cloned.1.call-start = ((), (), s32[]{:S(2)}) async-start(), calls=%async_computation.12 | async-start | bytes 14155776 | tf_op jit(solution)/shard_map/reduce_scatter | solution.py:217
  225.4 14.8 copy-start.2
  301.4 14.8 copy-start.2
  344.0 7.1 copy-start.3
  377.8 14.8 copy-start.2
  420.4 7.1 copy-start.3
  454.3 14.8 copy-start.2
  604.0 491.2 %reduce-scatter.21.cloned.1.call-start = ((), (), s32[]{:S(2)}) async-start(), calls=%async_computation.18 | async-start | bytes 18874368 | tf_op jit(solution)/shard_map/reduce_scatter | solution.py:220
  604.7 7.2 copy-start.10
  612.0 28.7 %copy-start.6 = (f32[512,4096]{1,0:T(8,128)}, f32[512,4096]{1,0:T(8,128)S(1)}, u32[]{:S(2)}) copy-start(f32[512,4096]{1,0:T(8,128)S(1)} %fusion.73) | copy-start | bytes 25165828
  661.5 716.1 %reduce-scatter.17.cloned.1.call-start = ((), (), s32[]{:S(2)}) async-start(), calls=%async_computation.16 | async-start | bytes 18874368 | tf_op jit(solution)/shard_map/reduce_scatter | solution.py:219
  672.0 423.4 %copy-start.29 = (bf16[1024]{0:T(1024)(128)(2,1)S(1)}, bf16[1024]{0:T(1024)(128)(2,1)}, u32[]{:S(2)}) copy-start(bf16[1024]{0:T(1024)(128)(2,1)} %param.28) | copy-start | bytes 6148
  672.0 423.4 %copy-start.30 = (bf16[1024]{0:T(1024)(128)(2,1)S(1)}, bf16[1024]{0:T(1024)(128)(2,1)}, u32[]{:S(2)}) copy-start(bf16[1024]{0:T(1024)(128)(2,1)} %param.32) | copy-start | bytes 6148
  672.0 767.9 %reduce-scatter.15.cloned.1.call-start = ((), (), s32[]{:S(2)}) async-start(), calls=%async_computation.15 | async-start | bytes 655360 | tf_op jit(solution)/shard_map/reduce_scatter | solution.py:224
  672.6 767.3 %reduce-scatter.11.cloned.1.call-start = ((), (), s32[]{:S(2)}) async-start(), calls=%async_computation.13 | async-start | bytes 1966080 | tf_op jit(solution)/shard_map/reduce_scatter | solution.py:223
  812.6 654.1 %reduce-scatter.23.cloned.1.call-start = ((), (), s32[]{:S(2)}) async-start(), calls=%async_computation.19 | async-start | bytes 2621440 | tf_op jit(solution)/shard_map/reduce_scatter | solution.py:226
  1095.3 405.7 %reduce-scatter.19.cloned.1.call-start = ((), (), s32[]{:S(2)}) async-start(), calls=%async_computation.17 | async-start | bytes 2621440 | tf_op jit(solution)/shard_map/reduce_scatter | solution.py:225
  1439.9 61.7 %copy-start.26 = (f32[1024]{0:T(1024)}, f32[1024]{0:T(1024)S(1)}, u32[]{:S(2)}) copy-start(f32[1024]{0:T(1024)S(1)} %get-tuple-element.511) | copy-start | bytes 12292
  (31 other events, 120.4 us)
Sparse Core Ops, SparseCore 0:
  210.3 89.3 reduce-scatter.12
  604.2 208.3 reduce-scatter.8
  816.4 278.8 reduce-scatter.20
  1098.9 278.6 reduce-scatter.16
  1380.5 20.7 reduce-scatter.14
  1404.3 28.1 reduce-scatter.10
  1435.5 31.1 reduce-scatter.22
  1469.8 31.1 reduce-scatter.18
where the time goes:
time: 1520 us; the launch traced here: 1510 us
  waiting for transfers between devices  810 us (53%)
  matrix products  334 us (22%)
  local copies, waits for them, and re-layouts  115 us (8%)
  other arithmetic  114 us (8%)
  blocking collectives  92.3 us (6%)
    reduce_scatter x1, waiting for transfers between devices, body(): lax.psum_scatter(matrices[3], 'dp', scatter_dimension=0, tiled=True)  283 us
    reduce_scatter x1, waiting for transfers between devices, body(): lax.psum_scatter(matrices[2], 'dp', scatter_dimension=0, tiled=True)  272 us
    reduce_scatter x1, waiting for transfers between devices, body(): lax.psum_scatter(matrices[0], 'dp', scatter_dimension=0, tiled=True)  140 us
    dot_general x4, matrix products, backward_block(): jnp.einsum('qhd,khd->hqk', grad_out_blk, values, preferred_element_type=j...  59.1 us
    dot_general x8, matrix products, block_scores(): jnp.einsum('qhd,khd->hqk', query_blk, keys_rot, preferred_element_type=jn...  54.1 us
    all_to_all x1, blocking collectives, body(): lax.all_to_all(grad_heads, 'head', split_axis=0, concat_axis=2, tiled=True)  51.9 us
    dynamic_update_slice x8, local copies, waits for them, and re-layouts, body(): lax.scan(backward_block, (zeros_kv, zeros_kv), jnp.arange(blocks, dtype=j...  49.8 us
    dot_general x4, matrix products, backward_block(): jnp.einsum('hqk,qhd->khd', probs_low, grad_out_blk, preferred_element_typ...  49.2 us
  transfers between devices with their start and end apart: 11, of which 7 were waited for; matrix products, arithmetic and copies ran while one was open for 35% of the time, Pallas kernels for 0%

commit v1 on v0

--- a/solution.py
+++ b/solution.py
@@ -97,9 +97,21 @@
     triple = (
         jnp.dot(norm_attn, w_qkv, preferred_element_type=jnp.float32) + b_qkv.astype(jnp.float32)
     ).astype(jnp.bfloat16)
-    triple_heads = lax.all_to_all(
-        triple.reshape(tok_rows, 3, width), "head", split_axis=2, concat_axis=0, tiled=True
-    )
+    x = triple.reshape(tok_rows, 3, width)
+    ways, here = (lax.axis_size("head"), lax.axis_index("head"))
+    width_2 = x.shape[2] // ways
+    dims = list(x.shape)
+    dims[2] = width_2
+    height = dims[0]
+    dims[0] = height * ways
+    triple_heads = jnp.zeros(dims, x.dtype)
+    for mask in range(ways):
+        part = lax.dynamic_slice_in_dim(x, (here ^ mask) * width_2, width_2, axis=2)
+        if mask:
+            part = lax.ppermute(part, "head", [(d, d ^ mask) for d in range(ways)])
+        triple_heads = lax.dynamic_update_slice_in_dim(
+            triple_heads, part, (here ^ mask) * height, axis=0
+        )
     group_rows = triple_heads.shape[0]
     local_width = triple_heads.shape[2]
     local_heads = local_width // HD

time: 1520 us -> 1470 us (0.967)
  waiting for transfers between devices: 810 us -> 787 us
    all_to_all x1 -> x0, waiting for transfers between devices: 45.1 us -> none  [body(): lax.all_to_all(triple.reshape(tok_rows, 3, width), 'head', split_axis=2,...]
    ppermute x0 -> x3, waiting for transfers between devices: none -> 22.6 us  [body(): part = lax.ppermute(part, 'head', [(d, d ^ mask) for d in range(ways)])]
  transfers between devices with their start and end apart: 11 -> 13, of which waited for: 7 -> 8; matrix products, arithmetic and copies ran while one was open for 35% -> 35% of each run, Pallas kernels for 0% -> 0%
where the time goes in v1:
time: 1470 us
  waiting for transfers between devices  787 us (54%)
  matrix products  334 us (23%)
  other arithmetic  109 us (7%)
  local copies, waits for them, and re-layouts  101 us (7%)
  blocking collectives  92.3 us (6%)
  between operations  15.2 us (1%)
    reduce_scatter x1, waiting for transfers between devices, body(): lax.psum_scatter(matrices[3], 'dp', scatter_dimension=0, tiled=True)  283 us
    reduce_scatter x1, waiting for transfers between devices, body(): lax.psum_scatter(matrices[2], 'dp', scatter_dimension=0, tiled=True)  272 us
    reduce_scatter x1, waiting for transfers between devices, body(): lax.psum_scatter(matrices[0], 'dp', scatter_dimension=0, tiled=True)  139 us
    dot_general x4, matrix products, backward_block(): jnp.einsum('qhd,khd->hqk', grad_out_blk, values, preferred_element_type=j...  59.1 us
    dot_general x8, matrix products, block_scores(): jnp.einsum('qhd,khd->hqk', query_blk, keys_rot, preferred_element_type=jn...  53.9 us
    all_to_all x1, blocking collectives, body(): lax.all_to_all(grad_heads, 'head', split_axis=0, concat_axis=2, tiled=True)  51.9 us
    dynamic_update_slice x8, local copies, waits for them, and re-layouts, body(): lax.scan(backward_block, (zeros_kv, zeros_kv), jnp.arange(blocks, dtype=j...  49.8 us
    dot_general x4, matrix products, backward_block(): jnp.einsum('hqk,qhd->khd', probs_low, grad_out_blk, preferred_element_typ...  49.2 us
  transfers between devices with their start and end apart: 13, of which 8 were waited for; matrix products, arithmetic and copies ran while one was open for 35% of the time, Pallas kernels for 0%

profile of v1, /device:TPU:0, one launch (start us, length us, event | category | flops | bytes accessed | tf_op | source)
XLA Modules:
  0.0 1465.3 jit_solution(12182415208427848532)
XLA Ops:
  52.8 14.4 collective-permute-done.2
  74.3 69.1 %while.27 = (s32[]{:T(128)}, bf16[4,512,4,64]{1,3,2,0:T(8,128)(2,1)}, f32[4,4,512]{2,1,0:T(4,128)S(1)}, s32[4]{0:T(128)S(1)}, s32[2048]{0:T(1024)S(1)}, /*index=...) while((s32[]{:T(128)}, ...), condition=%wide.region_8.9_spmd, body=%wide.region_5.0_spmd.sunk | while | flops 1127348736 | bytes 61426396 | solution.py:138
  167.4 306.0 %while.28 = (s32[]{:T(128)}, f32[2048,4,64]{0,2,1:T(8,128)}, f32[2048,4,64]{0,2,1:T(8,128)}, f32[4,512,4,64]{1,0,3,2:T(4,128)}, s32[4]{0:T(128)S(1)}, /*index=5*...) while((s32[]{:T(128)}, f32[2048,4,64]{0,2,1:T(8,128)}, ...), condition=%wide.region_11.12_spmd.clone, body=%wide.region_9.11_spmd.clone.sunk | while | flops 2753165824 | bytes 187246960 | solution.py:192
  182.4 14.8 %multiply_reduce_fusion.4 = (f32[4,512]{1,0:T(4,128)S(1)}, f32[4,512,2048]{2,1,0:T(8,128)}) fusion(f32[4,512,2048]{2,1,0:T(8,128)} %fusion.146, f32[4,512]{1,0:T(4,128)S(1)} %dynamic-slice_bitcast_fusion.2, pred[512,2048]{1,0:T(8,128)(4,1)} %fusion.147, bf16[2048,4,64]{0,2,1:T(8,128)(2,1)} %get-tuple-element.463, ...), kind=kOutput, calls=%fused_computation.19.clone.1 | convolution fusion | flops 557840384 | bytes 35930116 | tf_op jit(solution)/shard_map/while/body/eval_jaxpr/qhd,khd->hqk/dot_general | solution.py:175
  197.2 12.4 multiply_convert_fusion.3
  214.1 11.1 dynamic_update_slice.40
  231.8 12.1 fusion.149
  258.5 14.8 %multiply_reduce_fusion.4 = (f32[4,512]{1,0:T(4,128)S(1)}, f32[4,512,2048]{2,1,0:T(8,128)}) fusion(f32[4,512,2048]{2,1,0:T(8,128)} %fusion.146, f32[4,512]{1,0:T(4,128)S(1)} %dynamic-slice_bitcast_fusion.2, pred[512,2048]{1,0:T(8,128)(4,1)} %fusion.147, bf16[2048,4,64]{0,2,1:T(8,128)(2,1)} %get-tuple-element.463, ...), kind=kOutput, calls=%fused_computation.19.clone.1 | convolution fusion | flops 557840384 | bytes 35930116 | tf_op jit(solution)/shard_map/while/body/eval_jaxpr/qhd,khd->hqk/dot_general | solution.py:175
  273.2 12.1 multiply_convert_fusion.3
  308.0 12.4 fusion.149
  334.9 14.8 %multiply_reduce_fusion.4 = (f32[4,512]{1,0:T(4,128)S(1)}, f32[4,512,2048]{2,1,0:T(8,128)}) fusion(f32[4,512,2048]{2,1,0:T(8,128)} %fusion.146, f32[4,512]{1,0:T(4,128)S(1)} %dynamic-slice_bitcast_fusion.2, pred[512,2048]{1,0:T(8,128)(4,1)} %fusion.147, bf16[2048,4,64]{0,2,1:T(8,128)(2,1)} %get-tuple-element.463, ...), kind=kOutput, calls=%fused_computation.19.clone.1 | convolution fusion | flops 557840384 | bytes 35930116 | tf_op jit(solution)/shard_map/while/body/eval_jaxpr/qhd,khd->hqk/dot_general | solution.py:175
  349.7 12.1 multiply_convert_fusion.3
  384.5 12.4 fusion.149
  411.3 14.8 %multiply_reduce_fusion.4 = (f32[4,512]{1,0:T(4,128)S(1)}, f32[4,512,2048]{2,1,0:T(8,128)}) fusion(f32[4,512,2048]{2,1,0:T(8,128)} %fusion.146, f32[4,512]{1,0:T(4,128)S(1)} %dynamic-slice_bitcast_fusion.2, pred[512,2048]{1,0:T(8,128)(4,1)} %fusion.147, bf16[2048,4,64]{0,2,1:T(8,128)(2,1)} %get-tuple-element.463, ...), kind=kOutput, calls=%fused_computation.19.clone.1 | convolution fusion | flops 557840384 | bytes 35930116 | tf_op jit(solution)/shard_map/while/body/eval_jaxpr/qhd,khd->hqk/dot_general | solution.py:175
  426.1 12.1 multiply_convert_fusion.3
  460.9 12.4 fusion.149
  492.6 51.9 %all_to_all.50 = bf16[2048,3,256]{2,1,0:T(4,128)(2,1)S(1)} all-to-all(bf16[2048,3,256]{2,1,0:T(4,128)(2,1)} %copy.67), channel_id=1, replica_groups=mesh['dp'=8,'head'=4] {'head'}, dimensions={0} | all-to-all | bytes 6291456 | tf_op jit(solution)/shard_map/all_to_all | solution.py:202
  569.0 28.6 %convert_reduce_fusion = (f32[4096]{0:T(1024)S(1)}, bf16[512,4096]{1,0:T(8,128)(2,1)}, f32[512,4096]{1,0:T(8,128)}) fusion(f32[512,4096]{1,0:T(8,128)S(1)} %fusion.73, f32[4096]{0:T(1024)S(1)} %convert_element_type.119, bf16[512,1024]{1,0:T(8,128)(2,1)S(1)} %copy-done.12, bf16[4096,1024]{1,0:T(8,128)(2,1)} %param.31), kind=kOutput, calls=%fused_computation.49 | convolution fusion | flops 4452249600 | bytes 30441472 | tf_op jit(solution)/shard_map/td,fd->tf/dot_general | solution.py:153
  629.8 139.3 %reduce-scatter.9.cloned.1.call-done = f32[128,3072]{1,0:T(8,128)} async-done(((f32[1024,3072]{1,0:T(8,128)}), f32[128,3072]{1,0:T(8,128)}) %reduce-scatter.9.cloned.1.call-update) | async-done | bytes 1572880 | tf_op jit(solution)/shard_map/reduce_scatter | solution.py:229
  769.1 282.6 %reduce-scatter.21.cloned.1.call-done = f32[512,1024]{1,0:T(8,128)} async-done(((f32[4096,1024]{1,0:T(8,128)}), f32[512,1024]{1,0:T(8,128)}) %reduce-scatter.21.cloned.1.call-update) | async-done | bytes 2097168 | tf_op jit(solution)/shard_map/reduce_scatter | solution.py:232
  1062.3 271.7 %reduce-scatter.17.cloned.1.call-done = f32[128,4096]{1,0:T(8,128)} async-done(((f32[1024,4096]{1,0:T(8,128)}), f32[128,4096]{1,0:T(8,128)}) %reduce-scatter.17.cloned.1.call-update) | async-done | bytes 2097168 | tf_op jit(solution)/shard_map/reduce_scatter | solution.py:231
  1355.8 40.4 %all-reduce = (f32[1024]{0:T(1024)}, f32[1024]{0:T(1024)}, f32[1024]{0:T(1024)}, f32[1024]{0:T(1024)}, f32[3072]{0:T(1024)}, /*index=5*/f32[1024]{0:T(1024)S(1)}, f32[4096]{0:T(1024)}) all-reduce(f32[1024]{0:T(1024)S(1)} %get-tuple-element.170, f32[1024]{0:T(1024)S(1)} %get-tuple-element.175, ...), channel_id=1, replica_groups=mesh['dp'=8,'head'=4] {'dp','head'}, use_global_device_ids=true, to_apply=%region_17.18 | all-reduce | flops 12288 | bytes 98304 | tf_op jit(solution)/shard_map/psum | solution.py:215
  1396.3 26.8 %reduce-scatter.23.cloned.1.call-done = f32[512,256]{1,0:T(8,128)} async-done(((f32[512,1024]{1,0:T(8,128)}), f32[512,256]{1,0:T(8,128)}) %reduce-scatter.23.cloned.1.call-update) | async-done | bytes 524304 | tf_op jit(solution)/shard_map/reduce_scatter | solution.py:238
  1423.1 34.3 %reduce-scatter.19.cloned.1.call-done = f32[128,1024]{1,0:T(8,128)} async-done(((f32[128,4096]{1,0:T(8,128)}), f32[128,1024]{1,0:T(8,128)}) %reduce-scatter.19.cloned.1.call-update) | async-done | bytes 524304 | tf_op jit(solution)/shard_map/reduce_scatter | solution.py:237
  (263 shorter events, 378.1 us)
Async XLA Ops:
  7.2 24.9 %copy-start = (bf16[1024,1024]{1,0:T(8,128)(2,1)S(1)}, bf16[1024,1024]{1,0:T(8,128)(2,1)}, u32[]{:S(2)}) copy-start(bf16[1024,1024]{1,0:T(8,128)(2,1)} %param.27) | copy-start | bytes 6291460
  28.9 11.4 collective-permute-start
  29.4 21.2 %collective-permute-start.1 = (bf16[512,3,256]{0,2,1:T(8,128)(2,1)}, bf16[512,3,256]{0,2,1:T(8,128)(2,1)}, u32[]{:S(2)}, u32[]{:S(2)}) collective-permute-start(bf16[512,3,256]{0,2,1:T(8,128)(2,1)} %get-tuple-element.238), channel_id=1, source_target_pairs={{0,2},{1,3},{2,0},{3,1},{4,6},{5,7},{6,4},{7,5},{8,10},{9,11},{10,... | collective-permute-start | bytes 2359304 | tf_op jit(solution)/shard_map/ppermute | solution.py:111
  31.9 35.2 %collective-permute-start.2 = (bf16[512,3,256]{0,2,1:T(8,128)(2,1)S(1)}, bf16[512,3,256]{0,2,1:T(8,128)(2,1)}, u32[]{:S(2)}, u32[]{:S(2)}) collective-permute-start(bf16[512,3,256]{0,2,1:T(8,128)(2,1)S(1)} %get-tuple-element.237), channel_id=1, source_target_pairs={{0,3},{1,2},{2,1},{3,0},{4,7},{5,6},{6,5},{7,4},{8,11},{9,10},{10,... | collective-permute-start | bytes 2359304 | tf_op jit(solution)/shard_map/ppermute | solution.py:111
  34.4 109.0 %all-to-all-start.1 = ((bf16[512,4,256]{2,0,1:T(8,128)(2,1)}), bf16[512,4,256]{2,0,1:T(8,128)(2,1)}, u32[]{:S(2)}, u32[]{:S(2)}) async-start(bf16[512,4,256]{2,0,1:T(8,128)(2,1)} %bitcast.85), calls=%async_computation.1 | async-start | bytes 2097152 | tf_op jit(solution)/shard_map/all_to_all | solution.py:161
  40.3 32.8 %copy-start.14 = (f32[2048,8]{0,1:T(8,128)}, f32[2048,8]{0,1:T(8,128)S(1)}, u32[]{:S(2)}) copy-start(f32[2048,8]{0,1:T(8,128)S(1)} %get-tuple-element.257) | copy-start | bytes 196612
  143.5 19.1 %all-to-all-start = ((bf16[4,512,256]{1,2,0:T(8,128)(2,1)}), bf16[4,512,256]{1,2,0:T(8,128)(2,1)}, u32[]{:S(2)}, u32[]{:S(2)}) async-start(bf16[4,512,256]{1,2,0:T(8,128)(2,1)} %bitcast.12), calls=%async_computation | async-start | bytes 2097152 | tf_op jit(solution)/shard_map/all_to_all | solution.py:140
  147.7 481.4 %reduce-scatter.13.cloned.1.call-start = ((), (), s32[]{:S(2)}) async-start(), calls=%async_computation.13 | async-start | bytes 4718592 | tf_op jit(solution)/shard_map/reduce_scatter | solution.py:230
  167.4 601.6 %reduce-scatter.9.cloned.1.call-start = ((), (), s32[]{:S(2)}) async-start(), calls=%async_computation.11 | async-start | bytes 14155776 | tf_op jit(solution)/shard_map/reduce_scatter | solution.py:229
  182.4 14.8 %copy-start.2 = (pred[512,2048]{1,0:T(8,128)(4,1)S(1)}, pred[512,2048]{1,0:T(8,128)(4,1)}, u32[]{:S(2)}) copy-start(pred[512,2048]{1,0:T(8,128)(4,1)} %fusion.147) | copy-start | bytes 3145732 | tf_op jit(solution)/shard_map/while
  258.4 14.8 %copy-start.2 = (pred[512,2048]{1,0:T(8,128)(4,1)S(1)}, pred[512,2048]{1,0:T(8,128)(4,1)}, u32[]{:S(2)}) copy-start(pred[512,2048]{1,0:T(8,128)(4,1)} %fusion.147) | copy-start | bytes 3145732 | tf_op jit(solution)/shard_map/while
  334.9 14.8 %copy-start.2 = (pred[512,2048]{1,0:T(8,128)(4,1)S(1)}, pred[512,2048]{1,0:T(8,128)(4,1)}, u32[]{:S(2)}) copy-start(pred[512,2048]{1,0:T(8,128)(4,1)} %fusion.147) | copy-start | bytes 3145732 | tf_op jit(solution)/shard_map/while
  411.3 14.8 %copy-start.2 = (pred[512,2048]{1,0:T(8,128)(4,1)S(1)}, pred[512,2048]{1,0:T(8,128)(4,1)}, u32[]{:S(2)}) copy-start(pred[512,2048]{1,0:T(8,128)(4,1)} %fusion.147) | copy-start | bytes 3145732 | tf_op jit(solution)/shard_map/while
  561.1 490.6 %reduce-scatter.21.cloned.1.call-start = ((), (), s32[]{:S(2)}) async-start(), calls=%async_computation.17 | async-start | bytes 18874368 | tf_op jit(solution)/shard_map/reduce_scatter | solution.py:232
  561.8 7.2 copy-start.12
  569.0 28.6 %copy-start.8 = (f32[512,4096]{1,0:T(8,128)}, f32[512,4096]{1,0:T(8,128)S(1)}, u32[]{:S(2)}) copy-start(f32[512,4096]{1,0:T(8,128)S(1)} %fusion.73) | copy-start | bytes 25165828
  618.5 715.5 %reduce-scatter.17.cloned.1.call-start = ((), (), s32[]{:S(2)}) async-start(), calls=%async_computation.15 | async-start | bytes 18874368 | tf_op jit(solution)/shard_map/reduce_scatter | solution.py:231
  629.1 422.7 %copy-start.31 = (bf16[1024]{0:T(1024)(128)(2,1)S(1)}, bf16[1024]{0:T(1024)(128)(2,1)}, u32[]{:S(2)}) copy-start(bf16[1024]{0:T(1024)(128)(2,1)} %param.28) | copy-start | bytes 6148
  629.1 422.7 %copy-start.32 = (bf16[1024]{0:T(1024)(128)(2,1)S(1)}, bf16[1024]{0:T(1024)(128)(2,1)}, u32[]{:S(2)}) copy-start(bf16[1024]{0:T(1024)(128)(2,1)} %param.32) | copy-start | bytes 6148
  629.1 767.2 %reduce-scatter.15.cloned.1.call-start = ((), (), s32[]{:S(2)}) async-start(), calls=%async_computation.14 | async-start | bytes 655360 | tf_op jit(solution)/shard_map/reduce_scatter | solution.py:236
  629.7 766.6 %reduce-scatter.11.cloned.1.call-start = ((), (), s32[]{:S(2)}) async-start(), calls=%async_computation.12 | async-start | bytes 1966080 | tf_op jit(solution)/shard_map/reduce_scatter | solution.py:235
  769.0 654.1 %reduce-scatter.23.cloned.1.call-start = ((), (), s32[]{:S(2)}) async-start(), calls=%async_computation.18 | async-start | bytes 2621440 | tf_op jit(solution)/shard_map/reduce_scatter | solution.py:238
  1051.7 405.7 %reduce-scatter.19.cloned.1.call-start = ((), (), s32[]{:S(2)}) async-start(), calls=%async_computation.16 | async-start | bytes 2621440 | tf_op jit(solution)/shard_map/reduce_scatter | solution.py:237
  1396.3 61.8 %copy-start.28 = (f32[1024]{0:T(1024)}, f32[1024]{0:T(1024)S(1)}, u32[]{:S(2)}) copy-start(f32[1024]{0:T(1024)S(1)} %get-tuple-element.496) | copy-start | bytes 12292
  (35 other events, 142.6 us)
Sparse Core Ops, SparseCore 0:
  167.5 88.6 reduce-scatter.12
  561.2 207.7 reduce-scatter.8
  772.8 278.8 reduce-scatter.20
  1055.3 278.5 reduce-scatter.16
  1336.9 20.7 reduce-scatter.14
  1360.6 28.1 reduce-scatter.10
  1391.9 31.1 reduce-scatter.22
  1426.2 31.1 reduce-scatter.18
